TPU v7x, 32 devices: a whole 2x2x4 slice. The times are simulated.
32 devices in a mesh: dp: 8 (over y, x, core), mp: 4 (over z).
Axes of the slice: x: 2, y: 2, z: 4, core: 2. Of those that a mesh axis runs over, the one named last changes fastest.
Arguments:
- tokens: bfloat16 [12288, 4096], P('dp'), may hold values from -40 to 40
- norm_gain: bfloat16 [4096], replicated, may hold values from 0.099609375 to 1.8984375
- w_query: bfloat16 [4096, 2048], P(None, 'mp'), may hold values from -1 to 1
- w_key: bfloat16 [4096, 512], P(None, 'mp'), may hold values from -4 to 4
- w_value: bfloat16 [4096, 512], P(None, 'mp'), may hold values from -0.09375 to 0.09375
- w_out: bfloat16 [2048, 4096], P('mp'), may hold values from -0.125 to 0.125
- seq_starts: int32 [64], P('dp'), may hold values from 0 to 1408, as said below
- seq_lengths: int32 [64], P('dp'), may hold values from 128 to 640
- episode_ids: int32 [64], replicated, may hold values from 0 to 0, as said below
- class_ids: int32 [64], replicated, may hold values from 0 to 31
- query_flags: int32 [64], replicated, may hold values from 0 to 1
Outputs:
- log_probs: float32 [64, 32], P('dp')
- prototypes: float32 [32, 4096], P(None, 'mp')
Inputs may be any that keep to these rules, and one draw needn't show every extreme that they name: `seq_starts`: slot s lies in the buffer of dp index s // 8; the slots of one buffer are disjoint and in increasing order of start; start plus length is at most 1536, and in every draw the last slot of some buffer ends at row 1536. `episode_ids`: every class of every episode has at least one support sequence.
All inputs are finite; a program needn't handle non-finite values.
Results may differ from a plain program's by a relative error of at most 0.004.
Values sent between devices are 32-bit elements; how exact they have to be, the bound alone decides.
A program may use at most 128 MiB of HBM per device.

v0:
```python
import functools
import math

import numpy as np
import jax
import jax.numpy as jnp
from jax import lax
from jax.experimental import pallas as pl
from jax.experimental.pallas import tpu as pltpu
from jax.sharding import PartitionSpec as P

HEAD_DIM = 128
WAYS = 32
ROPE_BASE = 500000.0
NEG_FILL = -1e30
MESH = pl.DeviceIdType.MESH
F32 = jnp.float32
BF16 = jnp.bfloat16
HIGHEST = lax.Precision.HIGHEST


def pick(total, options):
    for candidate in options:
        if total % candidate == 0:
            return candidate
    return total


def encode_kernel(
    dims, st_ref, ln_ref, x_ref, gain_ref, wq_hbm, wk_hbm, wv_hbm, wo_hbm, cos_ref, sin_ref,
    hp_ref, ts_ref, w_s, wo_s, q_s, k_s, v_s, s_s, c_s, w_sem, wo_sem,
):
    rows, tile, qb, width, slots, heads, chunk, share, n_mp = dims
    hd = HEAD_DIM
    i = pl.program_id(0)
    last = pl.num_programs(0) - 1
    q_cols = heads * hd
    chunks = width // chunk
    rank = lax.axis_index("mp")
    wo_copy = pltpu.make_async_copy(wo_hbm, wo_s, wo_sem)

    def members(first, count):
        slot = lax.broadcasted_iota(jnp.int32, (slots, count), 0)
        token = lax.broadcasted_iota(jnp.int32, (slots, count), 1) + first
        lo = jnp.zeros((slots, count), jnp.int32)
        hi = jnp.zeros((slots, count), jnp.int32)
        for j in range(slots):
            lo = jnp.where(slot == j, st_ref[j], lo)
            hi = jnp.where(slot == j, st_ref[j] + ln_ref[j], hi)
        return jnp.where((token >= lo) & (token < hi), 1.0, 0.0).astype(BF16)

    @pl.when(i == 0)
    def _():
        def copies(c):
            r = pl.ds(c * chunk, chunk)
            return (
                pltpu.make_async_copy(wq_hbm.at[r, :], w_s.at[r, pl.ds(0, q_cols)], w_sem.at[c, 0]),
                pltpu.make_async_copy(wk_hbm.at[r, :], w_s.at[r, pl.ds(q_cols, hd)], w_sem.at[c, 1]),
                pltpu.make_async_copy(wv_hbm.at[r, :], w_s.at[r, pl.ds(q_cols + hd, hd)], w_sem.at[c, 2]),
            )

        for c in range(chunks):
            for copy in copies(c):
                copy.start()
        wo_copy.start()
        ts_ref[...] = jnp.zeros_like(ts_ref)
        c_s[...] = jnp.zeros_like(c_s)
        for c in range(chunks):
            for copy in copies(c):
                copy.wait()
            for b in range(chunk // 128):
                at = c * chunk + b * 128
                g = jnp.broadcast_to(gain_ref[at : at + 128].astype(F32)[None, :], (128, 128)).T
                for v in range(heads + 2):
                    w = w_s[at : at + 128, v * hd : (v + 1) * hd].astype(F32)
                    w_s[at : at + 128, v * hd : (v + 1) * hd] = (w * g).astype(BF16)

    half = tile // 2
    sums = []
    for b in range(2):
        acc = jnp.zeros((half, 128), F32)
        for v in range(width // 128):
            x = x_ref[b * half : (b + 1) * half, v * 128 : (v + 1) * 128].astype(F32)
            acc = acc + x * x
        sums.append(jnp.sum(acc, axis=-1, keepdims=True))
    rstd = lax.rsqrt(jnp.concatenate(sums, axis=0) / width + 1e-05)
    proj = jnp.dot(x_ref[...], w_s[...], preferred_element_type=F32)
    cos = cos_ref[...]
    sin = sin_ref[...]

    def rope(y):
        return (y * cos + pltpu.roll(y, hd // 2, 1) * sin).astype(BF16)

    q_rstd = rstd * (math.log2(math.e) / math.sqrt(hd))
    for h in range(heads):
        q_s[h] = rope(proj[:, h * hd : (h + 1) * hd] * q_rstd)
    here = pl.ds(pl.multiple_of(i * tile, tile), tile)
    k_s[here, :] = rope(proj[:, q_cols : q_cols + hd] * rstd)
    v_s[here, :] = (proj[:, q_cols + hd :] * rstd).astype(BF16)
    cols = pl.ds(pl.multiple_of(rank * share, share), share)
    ts_ref[...] += jnp.dot(members(i * tile, tile), x_ref[:, cols], preferred_element_type=F32)

    for b in range(tile // qb):
        block = i * (tile // qb) + b
        first = block * qb
        lo_row = first
        token = lax.broadcasted_iota(jnp.int32, (1, qb), 1) + first
        start = token
        for j in range(slots):
            s0 = st_ref[j]
            s1 = s0 + ln_ref[j]
            start = jnp.where((token >= s0) & (token < s1), s0, start)
            lo_row = jnp.where((first >= s0) & (first < s1), s0, lo_row)
        lo = lo_row // qb

        def fold(a, op):
            return op(a.reshape(qb // 8, 8, qb), axis=0)

        def score(kb, peaks):
            at = pl.ds(pl.multiple_of(kb * qb, qb), qb)
            keys = k_s[at, :]
            row = lax.broadcasted_iota(jnp.int32, (qb, qb), 0) + kb * qb
            ok = (row >= start) & (row <= token)
            out = []
            for h in range(heads):
                s = lax.dot_general(
                    keys, q_s[h, b * qb : (b + 1) * qb, :], (((1,), (1,)), ((), ())),
                    preferred_element_type=F32,
                )
                s = jnp.where(ok, s, NEG_FILL)
                s_s[at, h * qb : (h + 1) * qb] = s
                out.append(jnp.maximum(peaks[h], fold(s, jnp.max)))
            return tuple(out)

        peaks = lax.fori_loop(
            lo, block + 1, score, tuple(jnp.full((8, qb), NEG_FILL, F32) for _ in range(heads))
        )
        peaks = [jnp.max(p, axis=0, keepdims=True) for p in peaks]

        def expo(kb, totals):
            at = pl.ds(pl.multiple_of(kb * qb, qb), qb)
            out = []
            for h in range(heads):
                e = jnp.exp2(s_s[at, h * qb : (h + 1) * qb] - peaks[h])
                s_s[at, h * qb : (h + 1) * qb] = e
                out.append(totals[h] + fold(e, jnp.sum))
            return tuple(out)

        totals = lax.fori_loop(
            lo, block + 1, expo, tuple(jnp.zeros((8, qb), F32) for _ in range(heads))
        )
        inverse = [1.0 / jnp.sum(t, axis=0, keepdims=True) for t in totals]

        def gather(kb, carry):
            at = pl.ds(pl.multiple_of(kb * qb, qb), qb)
            for h in range(heads):
                part = c_s[h, at, :]
                for v in range(qb // 128):
                    e = s_s[at, h * qb + v * 128 : h * qb + (v + 1) * 128]
                    part = part + e * inverse[h][:, v * 128 : (v + 1) * 128]
                c_s[h, at, :] = part
            return carry

        lax.fori_loop(lo, block + 1, gather, 0)

    @pl.when(i == last)
    def _():
        member = members(0, rows)
        parts = []
        for h in range(heads):
            mass = jnp.sum(c_s[h], axis=-1, keepdims=True)
            mixed = mass * v_s[...].astype(F32)
            high = mixed.astype(BF16)
            low = (mixed - high.astype(F32)).astype(BF16)
            parts.append(
                jnp.dot(member, high, preferred_element_type=F32)
                + jnp.dot(member, low, preferred_element_type=F32)
            )
        attended = jnp.concatenate(parts, axis=-1)
        high = attended.astype(BF16)
        low = attended - high.astype(F32)
        both = jnp.concatenate([high.astype(F32), low], axis=0).astype(BF16)
        wo_copy.wait()
        for p in range(n_mp):
            w = wo_s[:, p * share : (p + 1) * share]
            out = jnp.dot(both, w, preferred_element_type=F32)
            hp_ref[p] = out[:slots] + out[slots:]


def exchange_kernel(
    dims, hp_ref, ts_ref, ln_ref, every_ref, gram_ref,
    rs_buf, ag_buf, g_buf, rs_send, rs_recv, ag_send, ag_recv, g_send, g_recv,
):
    n_dp, n_mp, slots, share, nseq, pieces, fold = dims
    dp = lax.axis_index("dp")
    mp = lax.axis_index("mp")
    barrier = pltpu.get_barrier_semaphore()
    for d in range(1, n_mp):
        pl.semaphore_signal(barrier, inc=1, device_id=(dp, lax.rem(mp + d, n_mp)), device_id_type=MESH)
    for d in range(1, n_dp):
        pl.semaphore_signal(barrier, inc=1, device_id=(lax.rem(dp + d, n_dp), mp), device_id_type=MESH)
    pl.semaphore_wait(barrier, n_mp + n_dp - 2)

    piece = share // pieces
    rs = {}
    for c in range(pieces):
        cols = pl.ds(c * piece, piece)
        for d in range(1, n_mp):
            peer = lax.rem(mp + d, n_mp)
            rs[c, d] = pltpu.make_async_remote_copy(
                src_ref=hp_ref.at[peer, :, cols], dst_ref=rs_buf.at[d - 1, c],
                send_sem=rs_send.at[c, d - 1], recv_sem=rs_recv.at[c, d - 1],
                device_id=(dp, peer), device_id_type=MESH,
            )
            rs[c, d].start()
    slot = lax.broadcasted_iota(jnp.int32, (slots, piece), 0)
    count = jnp.ones((slots, piece), F32)
    for j in range(slots):
        count = jnp.where(slot == j, ln_ref[j].astype(F32), count)
    own = pl.ds(pl.multiple_of(dp * slots, slots), slots)
    ag = {}
    for c in range(pieces):
        cols = slice(c * piece, (c + 1) * piece)
        pooled = ts_ref[:, cols] + hp_ref[mp, :, cols]
        for d in range(1, n_mp):
            rs[c, d].wait_recv()
            pooled = pooled + rs_buf[d - 1, c]
        ag_buf[c, own, :] = pooled / count
        for d in range(1, n_dp):
            peer = lax.rem(dp + d, n_dp)
            ag[c, d] = pltpu.make_async_remote_copy(
                src_ref=ag_buf.at[c, own, :], dst_ref=ag_buf.at[c, own, :],
                send_sem=ag_send.at[c, d - 1], recv_sem=ag_recv.at[c, d - 1],
                device_id=(peer, mp), device_id_type=MESH,
            )
            ag[c, d].start()
    part = None
    for c in range(pieces):
        for d in range(1, n_dp):
            ag[c, d].wait_recv()
        block = ag_buf[c]
        every_ref[:, c * piece : (c + 1) * piece] = block
        term = lax.dot_general(
            block, block, (((1,), (1,)), ((), ())), precision=HIGHEST, preferred_element_type=F32
        )
        part = term if part is None else part + term
    tall = nseq // fold
    g_buf[mp] = jnp.concatenate([part[f * tall : (f + 1) * tall] for f in range(fold)], axis=1)
    gs = {}
    for d in range(1, n_mp):
        peer = lax.rem(mp + d, n_mp)
        gs[d] = pltpu.make_async_remote_copy(
            src_ref=g_buf.at[mp], dst_ref=g_buf.at[mp], send_sem=g_send.at[d - 1],
            recv_sem=g_recv.at[d - 1], device_id=(dp, peer), device_id_type=MESH,
        )
        gs[d].start()
    for copy in list(rs.values()) + list(ag.values()):
        copy.wait_send()
    for d in range(1, n_mp):
        gs[d].wait_recv()
    gram = g_buf[0]
    for p in range(1, n_mp):
        gram = gram + g_buf[p]
    gram_ref[...] = jnp.concatenate(
        [gram[:, f * nseq : (f + 1) * nseq] for f in range(fold)], axis=0
    )
    for d in range(1, n_mp):
        gs[d].wait_send()


def score_kernel(dims, every_ref, gram_ref, ep_ref, cl_ref, fl_ref, lp_ref, pr_ref, d_buf):
    slots, width, nseq, classes = dims
    dp = lax.axis_index("dp")
    own = pl.ds(pl.multiple_of(dp * slots, slots), slots)
    every = every_ref[...]
    gram = gram_ref[...]
    label = ep_ref[...] * WAYS + cl_ref[...]
    support = fl_ref[...] == 0
    class_row = lax.broadcasted_iota(jnp.int32, (classes, nseq), 0)
    select = jnp.where((class_row == label) & support, 1.0, 0.0)
    a = lax.broadcasted_iota(jnp.int32, (slots, nseq), 0) + dp * slots
    mine = a == lax.broadcasted_iota(jnp.int32, (slots, nseq), 1)
    own_query = jnp.sum(jnp.where(mine, fl_ref[...].astype(F32), 0.0), axis=-1, keepdims=True)
    own_episode = jnp.sum(jnp.where(mine, ep_ref[...].astype(F32), 0.0), axis=-1, keepdims=True)
    eye = lax.broadcasted_iota(jnp.int32, (nseq, nseq), 0) == lax.broadcasted_iota(
        jnp.int32, (nseq, nseq), 1
    )
    diag = jnp.where(eye, gram, 0.0)
    scale_row = lax.rsqrt(jnp.sum(diag, axis=0, keepdims=True) / width + 1e-06)
    scale_col = lax.rsqrt(jnp.sum(diag, axis=1, keepdims=True) / width + 1e-06)
    gram = gram * scale_row * scale_col
    cross_t = jnp.dot(select, gram, precision=HIGHEST, preferred_element_type=F32)
    norm_col = jnp.maximum(jnp.sum(cross_t * select, axis=1, keepdims=True), 0.0)
    proto_col = lax.rsqrt(norm_col / width + 1e-06)
    sums = jnp.dot(select * scale_row, every, precision=HIGHEST, preferred_element_type=F32)
    pr_ref[...] = sums * proto_col

    d_buf[...] = gram
    mine_gram = d_buf[own, :]
    cross = lax.dot_general(
        mine_gram, select, (((1,), (1,)), ((), ())), precision=HIGHEST, preferred_element_type=F32
    )
    eye_c = lax.broadcasted_iota(jnp.int32, (classes, classes), 0) == lax.broadcasted_iota(
        jnp.int32, (classes, classes), 1
    )
    norm_row = jnp.sum(jnp.where(eye_c, norm_col, 0.0), axis=0, keepdims=True)
    proto_row = lax.rsqrt(norm_row / width + 1e-06)
    own_norm = jnp.sum(jnp.where(mine, mine_gram, 0.0), axis=-1, keepdims=True)
    distance = own_norm - 2.0 * (cross * proto_row) + norm_row * proto_row * proto_row
    picked = jnp.zeros((slots, WAYS), F32)
    for e in range(classes // WAYS):
        picked = jnp.where(own_episode == float(e), distance[:, e * WAYS : (e + 1) * WAYS], picked)
    logits = -picked / math.sqrt(width)
    shifted = logits - jnp.max(logits, axis=-1, keepdims=True)
    logp = shifted - jnp.log(jnp.sum(jnp.exp(shifted), axis=-1, keepdims=True))
    lp_ref[...] = jnp.where(own_query == 1.0, logp, 0.0)


def per_device(
    n_dp, n_mp, tokens, norm_gain, w_query, w_key, w_value, w_out,
    seq_starts, seq_lengths, episode_ids, class_ids, query_flags,
):
    rows, width = tokens.shape
    slots = seq_starts.shape[0]
    hd = HEAD_DIM
    heads = w_query.shape[1] // hd
    assert w_key.shape[1] == hd
    share = width // n_mp
    tile = pick(rows, (512, 256, 128))
    qb = pick(tile, (256, 128))
    chunk = pick(width, (512, 256, 128))
    frequency = ROPE_BASE ** (-np.arange(hd // 2, dtype=np.float64) * 2.0 / hd)
    angles = np.arange(rows, dtype=np.float64)[:, None] * frequency[None, :]
    cos = jnp.asarray(np.concatenate([np.cos(angles)] * 2, axis=1), F32)
    sin = jnp.asarray(np.concatenate([-np.sin(angles), np.sin(angles)], axis=1), F32)
    smem = pl.BlockSpec(memory_space=pltpu.SMEM)
    vmem = pl.BlockSpec(memory_space=pltpu.VMEM)
    hbm = pl.BlockSpec(memory_space=pl.ANY)
    dims = (rows, tile, qb, width, slots, heads, chunk, share, n_mp)
    head_part, token_sums = pl.pallas_call(
        functools.partial(encode_kernel, dims),
        grid=(rows // tile,),
        out_shape=(
            jax.ShapeDtypeStruct((n_mp, slots, share), F32),
            jax.ShapeDtypeStruct((slots, share), F32),
        ),
        in_specs=[
            smem, smem,
            pl.BlockSpec((tile, width), lambda i: (i, 0)),
            vmem,
            hbm, hbm, hbm, hbm,
            pl.BlockSpec((tile, hd), lambda i: (i, 0)),
            pl.BlockSpec((tile, hd), lambda i: (i, 0)),
        ],
        out_specs=(
            pl.BlockSpec((n_mp, slots, share), lambda i: (0, 0, 0)),
            pl.BlockSpec((slots, share), lambda i: (0, 0)),
        ),
        scratch_shapes=[
            pltpu.VMEM((width, (heads + 2) * hd), BF16),
            pltpu.VMEM(w_out.shape, BF16),
            pltpu.VMEM((heads, tile, hd), BF16),
            pltpu.VMEM((rows, hd), BF16),
            pltpu.VMEM((rows, hd), BF16),
            pltpu.VMEM((rows, heads * qb), F32),
            pltpu.VMEM((heads, rows, hd), F32),
            pltpu.SemaphoreType.DMA((width // chunk, 3)),
            pltpu.SemaphoreType.DMA,
        ],
        compiler_params=pltpu.CompilerParams(
            dimension_semantics=("arbitrary",), vmem_limit_bytes=60 * 1024 * 1024
        ),
    )(
        seq_starts, seq_lengths, tokens, norm_gain,
        w_query, w_key, w_value, w_out, cos, sin,
    )
    nseq = episode_ids.shape[0]
    episodes = max(1, nseq // (2 * WAYS))
    classes = episodes * WAYS
    dma = pltpu.SemaphoreType.DMA
    pieces = 2 if share % 256 == 0 else 1
    fold = 2 if nseq <= 64 else 1
    dims = (n_dp, n_mp, slots, share, nseq, pieces, fold)
    every, gram = pl.pallas_call(
        functools.partial(exchange_kernel, dims),
        out_shape=(
            jax.ShapeDtypeStruct((nseq, share), F32),
            jax.ShapeDtypeStruct((nseq, nseq), F32),
        ),
        in_specs=[vmem, vmem, smem],
        out_specs=(vmem, vmem),
        scratch_shapes=[
            pltpu.VMEM((n_mp - 1, pieces, slots, share // pieces), F32),
            pltpu.VMEM((pieces, nseq, share // pieces), F32),
            pltpu.VMEM((n_mp, nseq // fold, nseq * fold), F32),
            dma((pieces, n_mp - 1)), dma((pieces, n_mp - 1)),
            dma((pieces, n_dp - 1)), dma((pieces, n_dp - 1)),
            dma((n_mp - 1,)), dma((n_mp - 1,)),
        ],
        compiler_params=pltpu.CompilerParams(collective_id=0, has_side_effects=True),
    )(head_part, token_sums, seq_lengths)
    return pl.pallas_call(
        functools.partial(score_kernel, (slots, width, nseq, classes)),
        out_shape=(
            jax.ShapeDtypeStruct((slots, WAYS), F32),
            jax.ShapeDtypeStruct((classes, share), F32),
        ),
        in_specs=[vmem] * 5,
        out_specs=(vmem, vmem),
        scratch_shapes=[pltpu.VMEM((nseq, nseq), F32)],
    )(
        every, gram,
        episode_ids.reshape(1, nseq), class_ids.reshape(1, nseq), query_flags.reshape(1, nseq),
    )


def solution(mesh):
    placed = (
        P("dp", None), P(), P(None, "mp"), P(None, "mp"), P(None, "mp"), P("mp", None),
        P("dp"), P("dp"), P(), P(), P(),
    )
    return jax.shard_map(
        functools.partial(per_device, mesh.shape["dp"], mesh.shape["mp"]),
        mesh=mesh,
        in_specs=placed,
        out_specs=(P("dp", None), P(None, "mp")),
        check_vma=False,
    )
```

profile of v0, /device:TPU:0, one launch (start us, length us, event | category | flops | bytes accessed | tf_op | source)
XLA Modules:
  0.0 50.9 jit_solution(7118973296975335454)
XLA Ops:
  0.6 26.9 %shard_map.140 = (f32[4,8,1024]{2,1,0:T(8,128)}, f32[8,1024]{1,0:T(8,128)}) custom-call(s32[8]{0:T(128)} %st_ref.1, s32[8]{0:T(128)} %ln_ref.3, bf16[1536,4096]{1,0:T(8,128)(2,1)} %x_ref.1, bf16[4096]{0:T(1024)(128)(2,1)} %gain_ref.1, bf16[4096,512]{1,0:T(8,128)(2,1)} %wq_hbm.1, bf16[4096,128]{1,0:T(8,128)(2,1)} %wk_hbm.1, bf16[4096,128]{1,0:T(8,128)(2,1)} %wv_hbm.1, ...), custom_call_target="tpu_custom_call" | custom-call | tf_op jit(solution)/shard_map/pallas_call | solution.py:340
  27.6 21.2 %shard_map.141 = (f32[64,1024]{1,0:T(8,128)}, f32[64,64]{1,0:T(8,128)}) custom-call(f32[4,8,1024]{2,1,0:T(8,128)} %get-tuple-element.6.hp_ref, f32[8,1024]{1,0:T(8,128)} %get-tuple-element.7.ts_ref, s32[8]{0:T(128)} %ln_ref.3), custom_call_target="tpu_custom_call" | custom-call | tf_op jit(solution)/shard_map/pallas_call | solution.py:384
  48.8 2.1 %shard_map.142 = (f32[8,32]{1,0:T(8,128)}, f32[32,1024]{1,0:T(8,128)}) custom-call(f32[64,1024]{1,0:T(8,128)} %get-tuple-element.8.every_ref, f32[64,64]{1,0:T(8,128)} %get-tuple-element.9.gram_ref, s32[1,64]{1,0:T(1,128)} %bitcast.3, s32[1,64]{1,0:T(1,128)} %bitcast.4, s32[1,64]{1,0:T(1,128)} %bitcast.5), custom_call_target="tpu_custom_call" | custom-call | tf_op jit(solution)/shard_map/pallas_call | solution.py:402
where the time goes:
time: 50.3 us; the launch traced here: 50.9 us
  Pallas kernels  50.2 us (100%)
  between operations  0.65 us (1%)
    pallas_call x1, Pallas kernels, per_device(): pl.pallas_call(functools.partial(encode_kernel, dims), grid=(rows // tile...  26.9 us
    pallas_call x1, Pallas kernels, per_device(): pl.pallas_call(functools.partial(exchange_kernel, dims), out_shape=(jax.S...  21.2 us
    pallas_call x1, Pallas kernels, per_device(): pl.pallas_call(functools.partial(score_kernel, (slots, width, nseq, class...  2.12 us

commit v1 on v0

v1 whole, which is shorter than its diff:
```python
import functools
import math

import numpy as np
import jax
import jax.numpy as jnp
from jax import lax
from jax.experimental import pallas as pl
from jax.experimental.pallas import tpu as pltpu
from jax.sharding import PartitionSpec as P

HEAD_DIM = 128
WAYS = 32
ROPE_BASE = 500000.0
NEG_FILL = -1e30
MAX_LEN = 640
MIN_LEN = 128
QB = 128
MESH = pl.DeviceIdType.MESH
F32 = jnp.float32
BF16 = jnp.bfloat16
HIGHEST = lax.Precision.HIGHEST


def pick(total, options):
    for candidate in options:
        if total % candidate == 0:
            return candidate
    return total


def fused_kernel(
    dims, st_hbm, ln_hbm, gain_hbm, ep_hbm, cl_hbm, fl_hbm,
    x_hbm, wq_hbm, wk_hbm, wv_hbm, wo_hbm, trig_hbm,
    lp_ref, pr_ref, x_s, xg_s, w_s, wo_s, trig_s, qt_s, k_s, v_s, e_s, c_s, p_s, mx_s, ts_s,
    hp_s, rs_s, ag_s, ga_s, gb_s, st_ref, ln_ref, gain_ref, ep_ref, cl_ref, fl_ref,
    few_sem, x_sem, head_sem, w_sem, wo_sem, trig_sem,
    rs_send, rs_recv, ag_send, ag_recv, g_send, g_recv,
):
    rows, tile, width, slots, heads, chunk, share, n_mp, n_dp, classes = dims
    hd = HEAD_DIM
    i = pl.program_id(0)
    tiles = rows // tile
    q_cols = heads * hd
    chunks = width // chunk
    blocks = tile // QB
    slack = rows - MIN_LEN * slots

    def lowest(qb):
        first = qb * QB
        start = max(0, first - MAX_LEN + 1, MIN_LEN * ((first - slack) // MIN_LEN))
        return start // QB

    few = [
        pltpu.make_async_copy(src, dst, few_sem.at[k])
        for k, (src, dst) in enumerate((
            (gain_hbm, gain_ref), (st_hbm, st_ref), (ln_hbm, ln_ref),
            (ep_hbm, ep_ref), (cl_hbm, cl_ref), (fl_hbm, fl_ref),
        ))
    ]

    def head_copy(c):
        at = (pl.ds(0, tile), pl.ds(c * chunk, chunk))
        return pltpu.make_async_copy(x_hbm.at[at], x_s.at[at], head_sem.at[c])

    half = slots // 2
    near = n_dp * half
    dp = lax.axis_index("dp")
    rank = lax.axis_index("mp")
    wo_copy = pltpu.make_async_copy(wo_hbm, wo_s, wo_sem)
    trig_copy = pltpu.make_async_copy(trig_hbm, trig_s, trig_sem)

    def x_copy(t):
        r = pl.ds(t * tile, tile)
        return pltpu.make_async_copy(x_hbm.at[r, :], x_s.at[r, :], x_sem.at[t])

    def w_copies(c):
        r = pl.ds(c * chunk, chunk)
        return (
            pltpu.make_async_copy(wq_hbm.at[r, :], w_s.at[r, pl.ds(0, q_cols)], w_sem.at[c, 0]),
            pltpu.make_async_copy(wk_hbm.at[r, :], w_s.at[r, pl.ds(q_cols, hd)], w_sem.at[c, 1]),
            pltpu.make_async_copy(wv_hbm.at[r, :], w_s.at[r, pl.ds(q_cols + hd, hd)], w_sem.at[c, 2]),
        )

    def members(first, count):
        slot = lax.broadcasted_iota(jnp.int32, (slots, count), 0)
        token = lax.broadcasted_iota(jnp.int32, (slots, count), 1) + first
        lo = jnp.zeros((slots, count), jnp.int32)
        hi = jnp.zeros((slots, count), jnp.int32)
        for j in range(slots):
            lo = jnp.where(slot == j, st_ref[j], lo)
            hi = jnp.where(slot == j, st_ref[j] + ln_ref[j], hi)
        return jnp.where((token >= lo) & (token < hi), 1.0, 0.0).astype(BF16)

    def project(t):
        r0 = t * tile
        sums = [jnp.zeros((QB, 256), F32) for _ in range(blocks)]

        def scale(c):
            for b in range(blocks):
                r = slice(r0 + b * QB, r0 + (b + 1) * QB)
                for v in range(c * chunk, (c + 1) * chunk, 1024):
                    pair = []
                    for u in range(v, v + 1024, 256):
                        x = x_s[r, u : u + 256]
                        xg_s[b * QB : (b + 1) * QB, u : u + 256] = x * gain_ref[u : u + 256][None, :]
                        pair.append(x * x)
                    sums[b] = sums[b] + ((pair[0] + pair[1]) + (pair[2] + pair[3])).astype(F32)

        scale(0)
        for c in range(chunks):
            if t == 0:
                with jax.named_scope(f"wwait{c}"):
                    for copy in w_copies(c):
                        copy.wait()
                    if c + 1 < chunks:
                        head_copy(c + 1).wait()
                if c + 2 < chunks:
                    for copy in w_copies(c + 2):
                        copy.start()
                    if c + 3 < chunks:
                        head_copy(c + 3).start()
                if c + 2 == chunks - 1:
                    trig_copy.start()
                    x_copy(1).start()
            s = slice(c * chunk, (c + 1) * chunk)
            part = jnp.dot(xg_s[:, s], w_s[s, :], preferred_element_type=F32)
            p_s[...] = part if c == 0 else p_s[...] + part
            if c + 1 < chunks:
                scale(c + 1)
            yield
        if t == 0:
            trig_copy.wait()
            for copy in few[1:]:
                copy.wait()
        stats = [jnp.sum(a, axis=-1, keepdims=True) for a in sums]
        rstd = lax.rsqrt(jnp.concatenate(stats, axis=0) / width + 1e-05)
        cols = pl.ds(pl.multiple_of(rank * share, share), share)
        ts = jnp.dot(members(r0, tile), x_s[r0 : r0 + tile, cols], preferred_element_type=F32)
        if t == 0:
            ts_s[...] = ts
        else:
            ts_s[...] += ts
        trig = trig_s[r0 : r0 + tile, :]
        turned = pltpu.roll(trig, hd // 2, 1)
        front = lax.broadcasted_iota(jnp.int32, (tile, hd), 1) < hd // 2
        cos = jnp.where(front, trig, turned)
        sin = jnp.where(front, -turned, trig)

        def rope(y):
            return y * cos + pltpu.roll(y, hd // 2, 1) * sin

        q_rstd = rstd * (math.log2(math.e) / math.sqrt(hd))
        for h in range(heads):
            q = rope(p_s[:, h * hd : (h + 1) * hd] * q_rstd)
            for b in range(blocks):
                qt_s[t % 2, b, :, h * QB : (h + 1) * QB] = q[b * QB : (b + 1) * QB].T.astype(BF16)
        k_s[r0 : r0 + tile, :] = rope(p_s[:, q_cols : q_cols + hd] * rstd).astype(BF16)
        v_s[r0 : r0 + tile, :] = (p_s[:, q_cols + hd :] * rstd).astype(BF16)

    def mix(kb, h, part):
        r = slice(kb * QB, (kb + 1) * QB)
        mass = jnp.sum(part, axis=-1, keepdims=True)
        mx_s[r, h * hd : (h + 1) * hd] = (mass * v_s[r, :].astype(F32)).astype(BF16)

    def attend(t, mixed):
        scales = {}
        for b in range(blocks):
            qb = t * blocks + b
            first = qb * QB
            token = lax.broadcasted_iota(jnp.int32, (1, QB), 1) + first
            start = token
            for j in range(slots):
                s0 = st_ref[j]
                start = jnp.where((token >= s0) & (token < s0 + ln_ref[j]), s0, start)
            low = lowest(qb)
            peaks = {}
            totals = {}
            for kb in range(low, qb + 1):
                s_all = jnp.dot(
                    k_s[kb * QB : (kb + 1) * QB, :], qt_s[t % 2, b], preferred_element_type=F32
                )
                row = lax.broadcasted_iota(jnp.int32, (QB, QB), 0) + kb * QB
                ok = row >= start
                if kb == qb:
                    ok = ok & (row <= token)
                for h in range(heads):
                    s = jnp.where(ok, s_all[:, h * QB : (h + 1) * QB], NEG_FILL)
                    s = s.reshape(QB // 8, 8, QB)
                    peak = jnp.max(s, axis=0)
                    e = jnp.exp2(s - peak[None])
                    e_s[b, kb - low, h] = e.reshape(QB, QB)
                    peaks[kb, h] = peak
                    totals[kb, h] = jnp.sum(e, axis=0)
            for h in range(heads):
                top = peaks[low, h]
                for kb in range(low + 1, qb + 1):
                    top = jnp.maximum(top, peaks[kb, h])
                top = jnp.max(top, axis=0, keepdims=True)
                total = jnp.zeros((8, QB), F32)
                gain = {}
                for kb in range(low, qb + 1):
                    gain[kb] = jnp.exp2(peaks[kb, h] - top)
                    total = total + gain[kb] * totals[kb, h]
                inverse = 1.0 / jnp.sum(total, axis=0, keepdims=True)
                for kb in range(low, qb + 1):
                    scales[b, kb, h] = gain[kb] * inverse
            yield
        low0 = lowest(t * blocks)
        end0 = (t + 1) * blocks
        if mixed is not None:
            for kb in range(mixed, low0):
                for h in range(heads):
                    mix(kb, h, c_s[h, kb * QB : (kb + 1) * QB, :])
        for kb in range(low0, end0):
            if kb == (low0 + end0) // 2:
                yield
            for h in range(heads):
                r = slice(kb * QB, (kb + 1) * QB)
                part = None if kb >= t * blocks else c_s[h, r, :].reshape(QB // 8, 8, QB)
                for b in range(blocks):
                    if (b, kb, h) in scales:
                        low = lowest(t * blocks + b)
                        e = e_s[b, kb - low, h].reshape(QB // 8, 8, QB) * scales[b, kb, h][None]
                        part = e if part is None else part + e
                part = part.reshape(QB, QB)
                c_s[h, r, :] = part
                if mixed is not None and kb >= mixed:
                    mix(kb, h, part)

    bound = (rows - MIN_LEN * (slots - half), rows)
    floor = (0, MIN_LEN * half // QB)
    ready = (-(-bound[0] // tile) - 1, tiles - 1)

    def finish(p):
        low, high = floor[p] * QB, (ready[p] + 1) * tile
        attended = jnp.dot(
            members(low, high - low), mx_s[low:high, :], preferred_element_type=F32
        )
        upper = attended.astype(BF16)
        lower = attended - upper.astype(F32)
        both = jnp.concatenate([upper.astype(F32), lower], axis=0).astype(BF16)
        for m in range(n_mp):
            out = jnp.dot(both, wo_s[:, m * share : (m + 1) * share], preferred_element_type=F32)
            out = out[:slots] + out[slots:]
            hp_s[p, m] = out[p * half : (p + 1) * half]
            if m == n_mp // 2 - 1:
                yield

    def signal_all():
        barrier = pltpu.get_barrier_semaphore()
        for d in range(1, n_mp):
            peer = (dp, lax.rem(rank + d, n_mp))
            pl.semaphore_signal(barrier, inc=1, device_id=peer, device_id_type=MESH)
        for d in range(1, n_dp):
            peer = (lax.rem(dp + d, n_dp), rank)
            pl.semaphore_signal(barrier, inc=1, device_id=peer, device_id_type=MESH)

    def rs_copy(p, d):
        peer = lax.rem(rank + d, n_mp)
        return pltpu.make_async_remote_copy(
            src_ref=hp_s.at[p, peer], dst_ref=rs_s.at[p, d - 1],
            send_sem=rs_send.at[p, d - 1], recv_sem=rs_recv.at[p, d - 1],
            device_id=(dp, peer), device_id_type=MESH,
        )

    def ag_copy(p, d):
        return pltpu.make_async_remote_copy(
            src_ref=ag_s.at[p, dp], dst_ref=ag_s.at[p, dp],
            send_sem=ag_send.at[p, d - 1], recv_sem=ag_recv.at[p, d - 1],
            device_id=(lax.rem(dp + d, n_dp), rank), device_id_type=MESH,
        )

    def g_copy(p, d):
        ref = (ga_s, gb_s)[p]
        return pltpu.make_async_remote_copy(
            src_ref=ref.at[rank], dst_ref=ref.at[rank],
            send_sem=g_send.at[p, d - 1], recv_sem=g_recv.at[p, d - 1],
            device_id=(dp, lax.rem(rank + d, n_mp)), device_id_type=MESH,
        )

    def pool(p):
        with jax.named_scope(f"rs{p}"):
            for d in range(1, n_mp):
                rs_copy(p, d).wait_recv()
        slot = lax.broadcasted_iota(jnp.int32, (half, share), 0)
        count = jnp.ones((half, share), F32)
        for j in range(half):
            count = jnp.where(slot == j, ln_ref[p * half + j].astype(F32), count)
        pooled = ts_s[p * half : (p + 1) * half, :] + hp_s[p, rank]
        for d in range(1, n_mp):
            pooled = pooled + rs_s[p, d - 1]
        ag_s[p, dp] = pooled / count
        for d in range(1, n_dp):
            ag_copy(p, d).start()

    def split(a):
        upper = a.astype(BF16)
        return upper, (a - upper.astype(F32)).astype(BF16)

    def product(a, b, axes):
        (ah, al), (bh, bl) = a, b
        where = ((axes[:1], axes[1:]), ((), ()))
        def one(u, w):
            return lax.dot_general(u, w, where, preferred_element_type=F32)
        if al is None:
            return one(ah, bh) + one(ah, bl)
        return one(ah, bh) + (one(ah, bl) + one(al, bh))

    def gathered(p):
        with jax.named_scope(f"ag{p}"):
            for d in range(1, n_dp):
                ag_copy(p, d).wait_recv()
        return split(jnp.concatenate([ag_s[p, d] for d in range(n_dp)], axis=0))

    def folded(a):
        f = max(1, 128 // a.shape[1])
        tall = a.shape[0] // f
        return jnp.concatenate([a[k * tall : (k + 1) * tall] for k in range(f)], axis=1)

    def unfolded(ref, columns):
        total = ref[0]
        for m in range(1, n_mp):
            total = total + ref[m]
        f = total.shape[1] // columns
        return jnp.concatenate(
            [total[:, k * columns : (k + 1) * columns] for k in range(f)], axis=0
        )

    def tail():
        nseq = 2 * near
        for d in range(1, n_mp):
            rs_copy(1, d).start()
        pool(0)
        pool(1)
        place = lax.broadcasted_iota(jnp.int32, (nseq, nseq), 1)
        spot = place % near
        origin = (spot // half) * slots + (place // near) * half + spot % half
        order = jnp.where(
            lax.broadcasted_iota(jnp.int32, (nseq, nseq), 0) == origin, 1.0, 0.0
        ).astype(BF16)
        facts = jnp.concatenate(
            [ref[...].astype(F32).reshape(1, nseq) for ref in (ep_ref, cl_ref, fl_ref)]
            + [jnp.zeros((5, nseq), F32)], axis=0,
        ).astype(BF16)
        facts = jnp.dot(facts, order, preferred_element_type=F32)
        episode, label, query = facts[0:1], facts[1:2], facts[2:3]
        label = episode * float(WAYS) + label
        class_row = lax.broadcasted_iota(jnp.int32, (classes, nseq), 0).astype(F32)
        select = jnp.where((class_row == label) & (query == 0.0), 1.0, 0.0)
        a = lax.broadcasted_iota(jnp.int32, (slots, nseq), 0)
        a = (a // half) * near + dp * half + a % half
        mine = a == lax.broadcasted_iota(jnp.int32, (slots, nseq), 1)
        own_query = jnp.sum(jnp.where(mine, query, 0.0), axis=-1, keepdims=True)
        own_episode = jnp.sum(jnp.where(mine, episode, 0.0), axis=-1, keepdims=True)
        eye = lax.broadcasted_iota(jnp.int32, (nseq, nseq), 0) == lax.broadcasted_iota(
            jnp.int32, (nseq, nseq), 1
        )
        eye_c = lax.broadcasted_iota(jnp.int32, (classes, classes), 0) == lax.broadcasted_iota(
            jnp.int32, (classes, classes), 1
        )
        x0 = gathered(0)
        ga_s[rank] = folded(product(x0, x0, (1, 1)))
        for d in range(1, n_mp):
            g_copy(0, d).start()
        x1 = gathered(1)
        gb_s[rank] = folded(
            jnp.concatenate([product(x1, x0, (1, 1)), product(x1, x1, (1, 1))], axis=1)
        )
        for d in range(1, n_mp):
            g_copy(1, d).start()
        every = tuple(jnp.concatenate([u, w], axis=0) for u, w in zip(x0, x1))
        for p in range(2):
            for d in range(1, n_mp):
                rs_copy(p, d).wait_send()
            for d in range(1, n_dp):
                ag_copy(p, d).wait_send()
        with jax.named_scope("gwait"):
            for p in range(2):
                for d in range(1, n_mp):
                    g_copy(p, d).wait_recv()
        with jax.named_scope("score"):
            score(select, every, mine, eye, eye_c, own_query, own_episode)
        for p in range(2):
            for d in range(1, n_mp):
                g_copy(p, d).wait_send()

    def score(select, every, mine, eye, eye_c, own_query, own_episode):
        nseq = 2 * near
        g00 = unfolded(ga_s, near)
        below = unfolded(gb_s, nseq)
        gram = jnp.concatenate(
            [jnp.concatenate([g00, below[:, :near].T], axis=1), below], axis=0
        )
        diag = jnp.where(eye, gram, 0.0)
        norms = jnp.sum(diag, axis=0, keepdims=True)
        scale_row = lax.rsqrt(norms / width + 1e-06)
        norms = norms * scale_row * scale_row
        scale_col = lax.rsqrt(jnp.sum(diag, axis=1, keepdims=True) / width + 1e-06)
        gram = gram * scale_row * scale_col
        cross_t = product((select.astype(BF16), None), split(gram), (1, 0))
        norm_col = jnp.maximum(jnp.sum(cross_t * select, axis=1, keepdims=True), 0.0)
        proto_col = lax.rsqrt(norm_col / width + 1e-06)
        pr_ref[...] = product(split(select * scale_row), every, (1, 0)) * proto_col
        cross = product((mine.astype(F32).astype(BF16), None), split(cross_t), (1, 1))
        norm_row = jnp.sum(jnp.where(eye_c, norm_col, 0.0), axis=0, keepdims=True)
        proto_row = lax.rsqrt(norm_row / width + 1e-06)
        own_norm = jnp.sum(jnp.where(mine, norms, 0.0), axis=-1, keepdims=True)
        distance = own_norm - 2.0 * (cross * proto_row) + norm_row * proto_row * proto_row
        picked = jnp.zeros((slots, WAYS), F32)
        for e in range(classes // WAYS):
            picked = jnp.where(own_episode == float(e), distance[:, e * WAYS : (e + 1) * WAYS], picked)
        logits = -picked / math.sqrt(width)
        shifted = logits - jnp.max(logits, axis=-1, keepdims=True)
        logp = shifted - jnp.log(jnp.sum(jnp.exp(shifted), axis=-1, keepdims=True))
        lp_ref[...] = jnp.where(own_query == 1.0, logp, 0.0)

    for step in range(tiles + 1):
        @pl.when(i == step)
        def _(step=step):
            if step == 0:
                head_copy(0).start()
                few[0].start()
                for c in range(min(2, chunks)):
                    if c + 1 < chunks:
                        head_copy(c + 1).start()
                    for copy in w_copies(c):
                        copy.start()
                for copy in few[1:]:
                    copy.start()
                signal_all()
            if 0 < step < tiles - 1:
                x_copy(step + 1).start()
            if step == 2:
                wo_copy.start()
            if step < tiles:
                with jax.named_scope("xwait"):
                    if step == 0:
                        few[0].wait()
                        head_copy(0).wait()
                    else:
                        x_copy(step).wait()
            if step == ready[0] + 2:
                wo_copy.wait()
            with jax.named_scope(f"step{step}"):
                work = []
                if step < tiles:
                    work.append(project(step))
                if step == ready[0] + 2:
                    work.append(finish(0))
                if step > 0:
                    mixed = [floor[p] for p in range(2) if ready[p] == step - 1]
                    work.append(attend(step - 1, mixed[0] if mixed else None))
                while work:
                    work = [w for w in work if next(w, True) is None]
            if step == ready[0] + 2:
                with jax.named_scope("barrier"):
                    pl.semaphore_wait(pltpu.get_barrier_semaphore(), n_mp + n_dp - 2)
                for d in range(1, n_mp):
                    rs_copy(0, d).start()
            if step == tiles:
                with jax.named_scope("finish"):
                    for _ in finish(1):
                        pass
                with jax.named_scope("tail"):
                    tail()


def copy_kernel(a_ref, b_ref, x_ref, y_ref):
    x_ref[...] = a_ref[...]
    y_ref[...] = b_ref[...]


def per_device(
    n_dp, n_mp, tokens, norm_gain, w_query, w_key, w_value, w_out,
    seq_starts, seq_lengths, episode_ids, class_ids, query_flags,
):
    rows, width = tokens.shape
    slots = seq_starts.shape[0]
    hd = HEAD_DIM
    heads = w_query.shape[1] // hd
    assert w_key.shape[1] == hd
    share = width // n_mp
    tile = pick(rows, (256, 128))
    chunk = pick(width, (1024, 512, 256, 128))
    frequency = ROPE_BASE ** (-np.arange(hd // 2, dtype=np.float64) * 2.0 / hd)
    angles = np.arange(rows, dtype=np.float64)[:, None] * frequency[None, :]
    trig = jnp.asarray(np.concatenate([np.cos(angles), np.sin(angles)], axis=1), F32)
    vmem = pl.BlockSpec(memory_space=pltpu.VMEM)
    hbm = pl.BlockSpec(memory_space=pl.ANY)
    nseq = episode_ids.shape[0]
    classes = max(1, nseq // (2 * WAYS)) * WAYS
    half = slots // 2
    near = n_dp * half
    fold_a = max(1, 128 // near)
    fold_b = max(1, 128 // nseq)
    span = -(-(MAX_LEN - 1) // QB) + 1
    dma = pltpu.SemaphoreType.DMA
    dims = (rows, tile, width, slots, heads, chunk, share, n_mp, n_dp, classes)
    outs = pl.pallas_call(
        functools.partial(fused_kernel, dims),
        grid=(rows // tile + 1,),
        out_shape=(
            jax.ShapeDtypeStruct((slots, WAYS), F32),
            jax.ShapeDtypeStruct((classes, share), F32),
        ),
        in_specs=[hbm] * 12,
        out_specs=(
            pl.BlockSpec((slots, WAYS), lambda i: (0, 0)),
            pl.BlockSpec((classes, share), lambda i: (0, 0)),
        ),
        scratch_shapes=[
            pltpu.VMEM((rows, width), BF16),
            pltpu.VMEM((tile, width), BF16),
            pltpu.VMEM((width, (heads + 2) * hd), BF16),
            pltpu.VMEM(w_out.shape, BF16),
            pltpu.VMEM((rows, hd), F32),
            pltpu.VMEM((2, tile // QB, hd, heads * QB), BF16),
            pltpu.VMEM((rows, hd), BF16),
            pltpu.VMEM((rows, hd), BF16),
            pltpu.VMEM((tile // QB, span, heads, QB, QB), F32),
            pltpu.VMEM((heads, rows, QB), F32),
            pltpu.VMEM((tile, (heads + 2) * hd), F32),
            pltpu.VMEM((rows, heads * hd), BF16),
            pltpu.VMEM((slots, share), F32),
            pltpu.VMEM((2, n_mp, half, share), F32),
            pltpu.VMEM((2, n_mp - 1, half, share), F32),
            pltpu.VMEM((2, n_dp, half, share), F32),
            pltpu.VMEM((n_mp, near // fold_a, near * fold_a), F32),
            pltpu.VMEM((n_mp, near // fold_b, nseq * fold_b), F32),
            pltpu.SMEM((slots,), jnp.int32),
            pltpu.SMEM((slots,), jnp.int32),
            pltpu.VMEM((width,), BF16),
            pltpu.VMEM((nseq,), jnp.int32),
            pltpu.VMEM((nseq,), jnp.int32),
            pltpu.VMEM((nseq,), jnp.int32),
            dma((6,)),
            dma((rows // tile,)),
            dma((width // chunk,)),
            dma((width // chunk, 3)),
            dma,
            dma,
            dma((2, n_mp - 1)), dma((2, n_mp - 1)),
            dma((2, n_dp - 1)), dma((2, n_dp - 1)),
            dma((2, n_mp - 1)), dma((2, n_mp - 1)),
        ],
        compiler_params=pltpu.CompilerParams(
            dimension_semantics=("arbitrary",), vmem_limit_bytes=60 * 1024 * 1024,
            collective_id=0, has_side_effects=True,
        ),
    )(
        seq_starts, seq_lengths, norm_gain,
        episode_ids, class_ids, query_flags,
        tokens, w_query, w_key, w_value, w_out, trig,
    )
    return pl.pallas_call(
        copy_kernel,
        out_shape=tuple(jax.ShapeDtypeStruct(a.shape, a.dtype) for a in outs),
        in_specs=[vmem, vmem],
        out_specs=(vmem, vmem),
    )(*outs)


def solution(mesh):
    placed = (
        P("dp", None), P(), P(None, "mp"), P(None, "mp"), P(None, "mp"), P("mp", None),
        P("dp"), P("dp"), P(), P(), P(),
    )
    return jax.shard_map(
        functools.partial(per_device, mesh.shape["dp"], mesh.shape["mp"]),
        mesh=mesh,
        in_specs=placed,
        out_specs=(P("dp", None), P(None, "mp")),
        check_vma=False,
    )
```

time: 50.3 us -> 41.5 us (0.83); the launches traced: 50.9 us -> 41.3 us
  Pallas kernels: 50.2 us -> 40.6 us
    pallas_call x3 -> x2, Pallas kernels: 50.2 us -> 40.6 us  [the longest x1 39 us: per_device(): pl.pallas_call(functools.partial(fused_kernel, dims), grid=(rows // tile...]
where the time goes in v1:
time: 41.5 us; the launch traced here: 41.3 us
  Pallas kernels  40.6 us (98%)
  between operations  0.64 us (2%)
    pallas_call x1, Pallas kernels, per_device(): pl.pallas_call(functools.partial(fused_kernel, dims), grid=(rows // tile...  39 us
    pallas_call x1, Pallas kernels, per_device(): pl.pallas_call(copy_kernel, out_shape=tuple((jax.ShapeDtypeStruct(a.shape...  1.58 us

profile of v1, /device:TPU:0, one launch (start us, length us, event | category | flops | bytes accessed | tf_op | source)
XLA Modules:
  0.0 41.3 jit_solution(9912765720817391209)
XLA Ops:
  0.6 39.0 %shard_map.131 = (f32[8,32]{1,0:T(8,128)}, f32[32,1024]{1,0:T(8,128)}) custom-call(s32[8]{0:T(128)} %st_hbm.1, s32[8]{0:T(128)} %ln_hbm.1, bf16[4096]{0:T(1024)(128)(2,1)} %gain_hbm.1, s32[64]{0:T(128)} %ep_hbm.1, s32[64]{0:T(128)} %cl_hbm.1, s32[64]{0:T(128)} %fl_hbm.1, bf16[1536,4096]{1,0:T(8,128)(2,1)} %x_hbm.1, bf16[4096,512]{1,0:T(8,128)(2,1)} %wq_hbm.1, ...), custom_call_target="tpu_custom_call" | custom-call | tf_op jit(solution)/shard_map/pallas_call | solution.py:500
  39.7 1.6 %shard_map.132 = (f32[8,32]{1,0:T(8,128)}, f32[32,1024]{1,0:T(8,128)}) custom-call(f32[8,32]{1,0:T(8,128)} %get-tuple-element.4.a_ref, f32[32,1024]{1,0:T(8,128)} %get-tuple-element.5.b_ref), custom_call_target="tpu_custom_call" | custom-call | tf_op jit(solution)/shard_map/pallas_call | solution.py:556

commit v2 on v1

--- a/solution.py
+++ b/solution.py
@@ -37,7 +37,7 @@
     few_sem, x_sem, head_sem, w_sem, wo_sem, trig_sem,
     rs_send, rs_recv, ag_send, ag_recv, g_send, g_recv,
 ):
-    rows, tile, width, slots, heads, chunk, share, n_mp, n_dp, classes = dims
+    rows, tile, width, slots, heads, chunk, piece, share, n_mp, n_dp, classes = dims
     hd = HEAD_DIM
     i = pl.program_id(0)
     tiles = rows // tile
@@ -94,12 +94,14 @@
 
     def project(t):
         r0 = t * tile
+        span = chunk if t == 0 else piece
+        count = width // span
         sums = [jnp.zeros((QB, 256), F32) for _ in range(blocks)]
 
         def scale(c):
             for b in range(blocks):
                 r = slice(r0 + b * QB, r0 + (b + 1) * QB)
-                for v in range(c * chunk, (c + 1) * chunk, 1024):
+                for v in range(c * span, (c + 1) * span, 1024):
                     pair = []
                     for u in range(v, v + 1024, 256):
                         x = x_s[r, u : u + 256]
@@ -107,28 +109,28 @@
                         pair.append(x * x)
                     sums[b] = sums[b] + ((pair[0] + pair[1]) + (pair[2] + pair[3])).astype(F32)
 
-        scale(0)
-        for c in range(chunks):
+        for c in range(count if t == 0 else 1):
+            if t == 0 and c > 0:
+                head_copy(c).wait()
+            scale(c)
+        for c in range(count):
             if t == 0:
                 with jax.named_scope(f"wwait{c}"):
                     for copy in w_copies(c):
                         copy.wait()
-                    if c + 1 < chunks:
-                        head_copy(c + 1).wait()
-                if c + 2 < chunks:
-                    for copy in w_copies(c + 2):
+                if 0 < c and c + 1 < chunks:
+                    for copy in w_copies(c + 1):
                         copy.start()
-                    if c + 3 < chunks:
-                        head_copy(c + 3).start()
-                if c + 2 == chunks - 1:
+                if c == max(0, chunks - 2):
                     trig_copy.start()
                     x_copy(1).start()
-            s = slice(c * chunk, (c + 1) * chunk)
+            s = slice(c * span, (c + 1) * span)
             part = jnp.dot(xg_s[:, s], w_s[s, :], preferred_element_type=F32)
             p_s[...] = part if c == 0 else p_s[...] + part
-            if c + 1 < chunks:
+            if t > 0 and c + 1 < count:
                 scale(c + 1)
-            yield
+            for _ in range(4 // count):
+                yield
         if t == 0:
             trig_copy.wait()
             for copy in few[1:]:
@@ -234,18 +236,30 @@
 
     def finish(p):
         low, high = floor[p] * QB, (ready[p] + 1) * tile
+        if p == 0:
+            yield
+            yield
         attended = jnp.dot(
             members(low, high - low), mx_s[low:high, :], preferred_element_type=F32
         )
         upper = attended.astype(BF16)
         lower = attended - upper.astype(F32)
         both = jnp.concatenate([upper.astype(F32), lower], axis=0).astype(BF16)
-        for m in range(n_mp):
-            out = jnp.dot(both, wo_s[:, m * share : (m + 1) * share], preferred_element_type=F32)
-            out = out[:slots] + out[slots:]
-            hp_s[p, m] = out[p * half : (p + 1) * half]
-            if m == n_mp // 2 - 1:
-                yield
+        reach = list(range(1, n_mp))
+        reach.sort(key=lambda d: -min(d, n_mp - d))
+        reach.append(0)
+        for group in (reach[: n_mp // 2], reach[n_mp // 2 :]):
+            for d in group:
+                m = lax.rem(rank + d, n_mp)
+                cols = pl.ds(pl.multiple_of(m * share, share), share)
+                out = jnp.dot(both, wo_s[:, cols], preferred_element_type=F32)
+                out = out[:slots] + out[slots:]
+                hp_s[p, d] = out[p * half : (p + 1) * half]
+            if p == 1:
+                for d in group:
+                    if d > 0:
+                        rs_copy(p, d).start()
+            yield
 
     def signal_all():
         barrier = pltpu.get_barrier_semaphore()
@@ -259,16 +273,27 @@
     def rs_copy(p, d):
         peer = lax.rem(rank + d, n_mp)
         return pltpu.make_async_remote_copy(
-            src_ref=hp_s.at[p, peer], dst_ref=rs_s.at[p, d - 1],
+            src_ref=hp_s.at[p, d], dst_ref=rs_s.at[p, d - 1],
             send_sem=rs_send.at[p, d - 1], recv_sem=rs_recv.at[p, d - 1],
             device_id=(dp, peer), device_id_type=MESH,
         )
+
+    wide = 2 if n_dp % 4 == 0 else 1
+    tall = n_dp // (2 * wide)
+
+    def ag_peer(d):
+        k = n_dp - 1 - (d - 1)
+        c, x, y = k % 2, k // 2 % wide, k // (2 * wide)
+        chip = dp // 2
+        across = lax.rem(lax.rem(chip, wide) + x, wide)
+        down = lax.rem(chip // wide + y, tall)
+        return (down * wide + across) * 2 + lax.rem(lax.rem(dp, 2) + c, 2)
 
     def ag_copy(p, d):
         return pltpu.make_async_remote_copy(
             src_ref=ag_s.at[p, dp], dst_ref=ag_s.at[p, dp],
             send_sem=ag_send.at[p, d - 1], recv_sem=ag_recv.at[p, d - 1],
-            device_id=(lax.rem(dp + d, n_dp), rank), device_id_type=MESH,
+            device_id=(ag_peer(d), rank), device_id_type=MESH,
         )
 
     def g_copy(p, d):
@@ -287,7 +312,7 @@
         count = jnp.ones((half, share), F32)
         for j in range(half):
             count = jnp.where(slot == j, ln_ref[p * half + j].astype(F32), count)
-        pooled = ts_s[p * half : (p + 1) * half, :] + hp_s[p, rank]
+        pooled = ts_s[p * half : (p + 1) * half, :] + hp_s[p, 0]
         for d in range(1, n_mp):
             pooled = pooled + rs_s[p, d - 1]
         ag_s[p, dp] = pooled / count
@@ -329,8 +354,6 @@
 
     def tail():
         nseq = 2 * near
-        for d in range(1, n_mp):
-            rs_copy(1, d).start()
         pool(0)
         pool(1)
         place = lax.broadcasted_iota(jnp.int32, (nseq, nseq), 1)
@@ -419,13 +442,11 @@
         @pl.when(i == step)
         def _(step=step):
             if step == 0:
-                head_copy(0).start()
                 few[0].start()
-                for c in range(min(2, chunks)):
-                    if c + 1 < chunks:
-                        head_copy(c + 1).start()
-                    for copy in w_copies(c):
-                        copy.start()
+                for c in range(chunks):
+                    head_copy(c).start()
+                for copy in w_copies(0):
+                    copy.start()
                 for copy in few[1:]:
                     copy.start()
                 signal_all()
@@ -438,6 +459,9 @@
                     if step == 0:
                         few[0].wait()
                         head_copy(0).wait()
+                        if chunks > 1:
+                            for copy in w_copies(1):
+                                copy.start()
                     else:
                         x_copy(step).wait()
             if step == ready[0] + 2:
@@ -482,7 +506,8 @@
     assert w_key.shape[1] == hd
     share = width // n_mp
     tile = pick(rows, (256, 128))
-    chunk = pick(width, (1024, 512, 256, 128))
+    chunk = pick(width, (2048, 512, 256, 128))
+    piece = pick(width, (1024, 512, 256, 128))
     frequency = ROPE_BASE ** (-np.arange(hd // 2, dtype=np.float64) * 2.0 / hd)
     angles = np.arange(rows, dtype=np.float64)[:, None] * frequency[None, :]
     trig = jnp.asarray(np.concatenate([np.cos(angles), np.sin(angles)], axis=1), F32)
@@ -496,7 +521,7 @@
     fold_b = max(1, 128 // nseq)
     span = -(-(MAX_LEN - 1) // QB) + 1
     dma = pltpu.SemaphoreType.DMA
-    dims = (rows, tile, width, slots, heads, chunk, share, n_mp, n_dp, classes)
+    dims = (rows, tile, width, slots, heads, chunk, piece, share, n_mp, n_dp, classes)
     outs = pl.pallas_call(
         functools.partial(fused_kernel, dims),
         grid=(rows // tile + 1,),

time: 41.5 us -> 40.3 us (0.971)
  Pallas kernels: 40.6 us -> 39.4 us
    pallas_call x1, Pallas kernels: 39 us -> 37.9 us  [per_device(): pl.pallas_call(functools.partial(fused_kernel, dims), grid=(rows // tile...]
where the time goes in v2:
time: 40.3 us; the launch traced here: 40.1 us
  Pallas kernels  39.4 us (98%)
  between operations  0.64 us (2%)
    pallas_call x1, Pallas kernels, per_device(): pl.pallas_call(functools.partial(fused_kernel, dims), grid=(rows // tile...  37.9 us
    pallas_call x1, Pallas kernels, per_device(): pl.pallas_call(copy_kernel, out_shape=tuple((jax.ShapeDtypeStruct(a.shape...  1.58 us

profile of v2, /device:TPU:0, one launch (start us, length us, event | category | flops | bytes accessed | tf_op | source)
XLA Modules:
  0.0 40.1 jit_solution(10382637841738735014)
XLA Ops:
  0.6 37.9 %shard_map.131 = (f32[8,32]{1,0:T(8,128)}, f32[32,1024]{1,0:T(8,128)}) custom-call(s32[8]{0:T(128)} %st_hbm.1, s32[8]{0:T(128)} %ln_hbm.1, bf16[4096]{0:T(1024)(128)(2,1)} %gain_hbm.1, s32[64]{0:T(128)} %ep_hbm.1, s32[64]{0:T(128)} %cl_hbm.1, s32[64]{0:T(128)} %fl_hbm.1, bf16[1536,4096]{1,0:T(8,128)(2,1)} %x_hbm.1, bf16[4096,512]{1,0:T(8,128)(2,1)} %wq_hbm.1, ...), custom_call_target="tpu_custom_call" | custom-call | tf_op jit(solution)/shard_map/pallas_call | solution.py:525
  38.5 1.6 %shard_map.132 = (f32[8,32]{1,0:T(8,128)}, f32[32,1024]{1,0:T(8,128)}) custom-call(f32[8,32]{1,0:T(8,128)} %get-tuple-element.4.a_ref, f32[32,1024]{1,0:T(8,128)} %get-tuple-element.5.b_ref), custom_call_target="tpu_custom_call" | custom-call | tf_op jit(solution)/shard_map/pallas_call | solution.py:581

commit v3 on v2

--- a/solution.py
+++ b/solution.py
@@ -32,7 +32,7 @@
 def fused_kernel(
     dims, st_hbm, ln_hbm, gain_hbm, ep_hbm, cl_hbm, fl_hbm,
     x_hbm, wq_hbm, wk_hbm, wv_hbm, wo_hbm, trig_hbm,
-    lp_ref, pr_ref, x_s, xg_s, w_s, wo_s, trig_s, qt_s, k_s, v_s, e_s, c_s, p_s, mx_s, ts_s,
+    lp_ref, pr_ref, x_s, xg_s, w_s, wo_s, trig_s, qt_s, k_s, v_s, e_s, c_s, p_s, sq_s, mx_s, ts_s,
     hp_s, rs_s, ag_s, ga_s, gb_s, st_ref, ln_ref, gain_ref, ep_ref, cl_ref, fl_ref,
     few_sem, x_sem, head_sem, w_sem, wo_sem, trig_sem,
     rs_send, rs_recv, ag_send, ag_recv, g_send, g_recv,
@@ -44,6 +44,7 @@
     q_cols = heads * hd
     chunks = width // chunk
     blocks = tile // QB
+    far = sorted(range(1, n_mp), key=lambda d: -min(d, n_mp - d))
     slack = rows - MIN_LEN * slots
 
     def lowest(qb):
@@ -60,7 +61,7 @@
     ]
 
     def head_copy(c):
-        at = (pl.ds(0, tile), pl.ds(c * chunk, chunk))
+        at = (pl.ds(0, tile), pl.ds(pl.multiple_of(c * chunk, chunk), chunk))
         return pltpu.make_async_copy(x_hbm.at[at], x_s.at[at], head_sem.at[c])
 
     half = slots // 2
@@ -68,14 +69,17 @@
     dp = lax.axis_index("dp")
     rank = lax.axis_index("mp")
     wo_copy = pltpu.make_async_copy(wo_hbm, wo_s, wo_sem)
-    trig_copy = pltpu.make_async_copy(trig_hbm, trig_s, trig_sem)
+
+    def trig_copy(k):
+        r = pl.ds(0, tile) if k == 0 else pl.ds(tile, rows - tile)
+        return pltpu.make_async_copy(trig_hbm.at[r, :], trig_s.at[r, :], trig_sem.at[k])
 
     def x_copy(t):
         r = pl.ds(t * tile, tile)
         return pltpu.make_async_copy(x_hbm.at[r, :], x_s.at[r, :], x_sem.at[t])
 
     def w_copies(c):
-        r = pl.ds(c * chunk, chunk)
+        r = pl.ds(pl.multiple_of(c * chunk, chunk), chunk)
         return (
             pltpu.make_async_copy(wq_hbm.at[r, :], w_s.at[r, pl.ds(0, q_cols)], w_sem.at[c, 0]),
             pltpu.make_async_copy(wk_hbm.at[r, :], w_s.at[r, pl.ds(q_cols, hd)], w_sem.at[c, 1]),
@@ -109,32 +113,58 @@
                         pair.append(x * x)
                     sums[b] = sums[b] + ((pair[0] + pair[1]) + (pair[2] + pair[3])).astype(F32)
 
-        for c in range(count if t == 0 else 1):
-            if t == 0 and c > 0:
+        if t == 0:
+            def chunk_step(c, carry):
+                off = pl.multiple_of(c * chunk, chunk)
                 head_copy(c).wait()
-            scale(c)
-        for c in range(count):
-            if t == 0:
-                with jax.named_scope(f"wwait{c}"):
-                    for copy in w_copies(c):
-                        copy.wait()
-                if 0 < c and c + 1 < chunks:
-                    for copy in w_copies(c + 1):
+                gain = gain_ref[pl.ds(off, chunk)]
+                for b in range(blocks):
+                    r = slice(b * QB, (b + 1) * QB)
+                    total = sq_s[b]
+                    for v in range(0, chunk, 1024):
+                        pair = []
+                        for u in range(v, v + 1024, 256):
+                            cols = pl.ds(off + u, 256)
+                            x = x_s[r, cols]
+                            xg_s[r, cols] = x * gain[u : u + 256][None, :]
+                            pair.append(x * x)
+                        total = total + ((pair[0] + pair[1]) + (pair[2] + pair[3])).astype(F32)
+                    sq_s[b] = total
+                for copy in w_copies(c):
+                    copy.wait()
+
+                @pl.when(c + 3 < chunks)
+                def _():
+                    for copy in w_copies(c + 3):
                         copy.start()
-                if c == max(0, chunks - 2):
-                    trig_copy.start()
+
+                @pl.when(c + 2 == chunks)
+                def _():
                     x_copy(1).start()
+                    trig_copy(1).start()
+
+                s = pl.ds(off, chunk)
+                p_s[...] += jnp.dot(xg_s[:, s], w_s[s, :], preferred_element_type=F32)
+                return carry
+
+            with jax.named_scope("first"):
+                lax.fori_loop(0, chunks, chunk_step, 0)
+            sums = [sq_s[b] for b in range(blocks)]
+        else:
+            scale(0)
+        for c in range(count if t > 0 else 0):
             s = slice(c * span, (c + 1) * span)
             part = jnp.dot(xg_s[:, s], w_s[s, :], preferred_element_type=F32)
             p_s[...] = part if c == 0 else p_s[...] + part
-            if t > 0 and c + 1 < count:
+            if c + 1 < count:
                 scale(c + 1)
             for _ in range(4 // count):
                 yield
         if t == 0:
-            trig_copy.wait()
-            for copy in few[1:]:
-                copy.wait()
+            with jax.named_scope("trig"):
+                trig_copy(0).wait()
+                for copy in few[1:]:
+                    copy.wait()
         stats = [jnp.sum(a, axis=-1, keepdims=True) for a in sums]
         rstd = lax.rsqrt(jnp.concatenate(stats, axis=0) / width + 1e-05)
         cols = pl.ds(pl.multiple_of(rank * share, share), share)
@@ -245,9 +275,7 @@
         upper = attended.astype(BF16)
         lower = attended - upper.astype(F32)
         both = jnp.concatenate([upper.astype(F32), lower], axis=0).astype(BF16)
-        reach = list(range(1, n_mp))
-        reach.sort(key=lambda d: -min(d, n_mp - d))
-        reach.append(0)
+        reach = far + [0]
         for group in (reach[: n_mp // 2], reach[n_mp // 2 :]):
             for d in group:
                 m = lax.rem(rank + d, n_mp)
@@ -384,13 +412,13 @@
         )
         x0 = gathered(0)
         ga_s[rank] = folded(product(x0, x0, (1, 1)))
-        for d in range(1, n_mp):
+        for d in far:
             g_copy(0, d).start()
         x1 = gathered(1)
         gb_s[rank] = folded(
             jnp.concatenate([product(x1, x0, (1, 1)), product(x1, x1, (1, 1))], axis=1)
         )
-        for d in range(1, n_mp):
+        for d in far:
             g_copy(1, d).start()
         every = tuple(jnp.concatenate([u, w], axis=0) for u, w in zip(x0, x1))
         for p in range(2):
@@ -445,8 +473,12 @@
                 few[0].start()
                 for c in range(chunks):
                     head_copy(c).start()
-                for copy in w_copies(0):
-                    copy.start()
+                for c in range(min(3, chunks)):
+                    for copy in w_copies(c):
+                        copy.start()
+                trig_copy(0).start()
+                p_s[...] = jnp.zeros_like(p_s)
+                sq_s[...] = jnp.zeros_like(sq_s)
                 for copy in few[1:]:
                     copy.start()
                 signal_all()
@@ -458,12 +490,10 @@
                 with jax.named_scope("xwait"):
                     if step == 0:
                         few[0].wait()
-                        head_copy(0).wait()
-                        if chunks > 1:
-                            for copy in w_copies(1):
-                                copy.start()
                     else:
                         x_copy(step).wait()
+                    if step == 1:
+                        trig_copy(1).wait()
             if step == ready[0] + 2:
                 wo_copy.wait()
             with jax.named_scope(f"step{step}"):
@@ -506,7 +536,7 @@
     assert w_key.shape[1] == hd
     share = width // n_mp
     tile = pick(rows, (256, 128))
-    chunk = pick(width, (2048, 512, 256, 128))
+    chunk = pick(width, (1024, 512, 256, 128))
     piece = pick(width, (1024, 512, 256, 128))
     frequency = ROPE_BASE ** (-np.arange(hd // 2, dtype=np.float64) * 2.0 / hd)
     angles = np.arange(rows, dtype=np.float64)[:, None] * frequency[None, :]
@@ -546,6 +576,7 @@
             pltpu.VMEM((tile // QB, span, heads, QB, QB), F32),
             pltpu.VMEM((heads, rows, QB), F32),
             pltpu.VMEM((tile, (heads + 2) * hd), F32),
+            pltpu.VMEM((tile // QB, QB, 256), F32),
             pltpu.VMEM((rows, heads * hd), BF16),
             pltpu.VMEM((slots, share), F32),
             pltpu.VMEM((2, n_mp, half, share), F32),
@@ -564,7 +595,7 @@
             dma((width // chunk,)),
             dma((width // chunk, 3)),
             dma,
-            dma,
+            dma((2,)),
             dma((2, n_mp - 1)), dma((2, n_mp - 1)),
             dma((2, n_dp - 1)), dma((2, n_dp - 1)),
             dma((2, n_mp - 1)), dma((2, n_mp - 1)),

time: 40.3 us -> 40.2 us (level)
  no operation moved by 1% of the time
where the time goes in v3:
time: 40.2 us; the launch traced here: 40 us
  Pallas kernels  39.4 us (98%)
  between operations  0.64 us (2%)
    pallas_call x1, Pallas kernels, per_device(): pl.pallas_call(functools.partial(fused_kernel, dims), grid=(rows // tile...  37.8 us
    pallas_call x1, Pallas kernels, per_device(): pl.pallas_call(copy_kernel, out_shape=tuple((jax.ShapeDtypeStruct(a.shape...  1.58 us

profile of v3, /device:TPU:0, one launch (start us, length us, event | category | flops | bytes accessed | tf_op | source)
XLA Modules:
  0.0 40.0 jit_solution(3247376892247273013)
XLA Ops:
  0.6 37.8 %shard_map.131 = (f32[8,32]{1,0:T(8,128)}, f32[32,1024]{1,0:T(8,128)}) custom-call(s32[8]{0:T(128)} %st_hbm.1, s32[8]{0:T(128)} %ln_hbm.1, bf16[4096]{0:T(1024)(128)(2,1)} %gain_hbm.1, s32[64]{0:T(128)} %ep_hbm.1, s32[64]{0:T(128)} %cl_hbm.1, s32[64]{0:T(128)} %fl_hbm.1, bf16[1536,4096]{1,0:T(8,128)(2,1)} %x_hbm.1, bf16[4096,512]{1,0:T(8,128)(2,1)} %wq_hbm.1, ...), custom_call_target="tpu_custom_call" | custom-call | tf_op jit(solution)/shard_map/pallas_call | solution.py:555
  38.5 1.6 %shard_map.132 = (f32[8,32]{1,0:T(8,128)}, f32[32,1024]{1,0:T(8,128)}) custom-call(f32[8,32]{1,0:T(8,128)} %get-tuple-element.4.a_ref, f32[32,1024]{1,0:T(8,128)} %get-tuple-element.5.b_ref), custom_call_target="tpu_custom_call" | custom-call | tf_op jit(solution)/shard_map/pallas_call | solution.py:612
